TPU v7x, 32 devices: a whole 2x2x4 slice. The times are simulated.
32 devices in a mesh: dp: 8 (over y, x, core), tensor: 4 (over z).
Axes of the slice: x: 2, y: 2, z: 4, core: 2. Of those that a mesh axis runs over, the one named last changes fastest.
Arguments:
- attn_out: bfloat16 [3072, 4096], P('dp', 'tensor'), may hold values from -24 to 24
- out_grad: bfloat16 [3072, 4096], P('dp', 'tensor'), may hold values from -6 to 6
- proj_in: bfloat16 [64, 4096], P(None, 'tensor'), may hold values from -0.09375 to 0.09375
- proj_out: bfloat16 [64, 4096], P(None, 'tensor'), may hold values from -0.09375 to 0.09375
- targets: float32 [256, 64, 64], P(None, 'tensor'), may hold values from -6 to 6
Outputs:
- scores: float32 [48, 256], P('dp')
All inputs are finite; a program needn't handle non-finite values.
Results may differ from a plain program's by a relative error of at most 0.0015.
Values sent between devices are 32-bit elements; how exact they have to be, the bound alone decides.
A program may use at most 64 MiB of HBM per device.

v0:
```python
import jax
import jax.numpy as jnp
from jax import lax
from jax.sharding import PartitionSpec as P

LEN = 64


damping_ratio = 0.5
epsilon = 1e-06


def inner_rows(left, right):
    return lax.dot_general(
        left,
        right,
        (((1,), (1,)), ((), ())),
        precision=lax.Precision.HIGHEST,
        preferred_element_type=jnp.float32,
    )


def shards(attn_out, out_grad, proj_in, proj_out, targets):
    tok_rows = attn_out.shape[0]
    proj_rank = proj_in.shape[0]
    seq_count = tok_rows // LEN
    inputs_part = jnp.einsum("td,rd->tr", attn_out, proj_in, preferred_element_type=jnp.float32)
    grads_part = jnp.einsum("td,rd->tr", out_grad, proj_out, preferred_element_type=jnp.float32)
    inputs_low = lax.psum_scatter(inputs_part, "tensor", scatter_dimension=1, tiled=True)
    grads_low = lax.psum(grads_part, "tensor")
    part_width = inputs_low.shape[1]
    sample_grads = jnp.einsum(
        "sti,sto->sio",
        inputs_low.reshape(seq_count, LEN, part_width),
        grads_low.reshape(seq_count, LEN, proj_rank),
        precision=lax.Precision.HIGHEST,
    ).reshape(seq_count, part_width * proj_rank)
    target_rows = targets.reshape(targets.shape[0], part_width * proj_rank)
    gathered = lax.all_gather(sample_grads, "dp", axis=0, tiled=True)
    gram_matrix = inner_rows(gathered, gathered)
    cross_terms = inner_rows(gathered, target_rows)
    gram_matrix, cross_terms = lax.psum((gram_matrix, cross_terms), "tensor")
    trace_sum = jnp.trace(gram_matrix)
    samples = gram_matrix.shape[0]
    damping = damping_ratio * trace_sum / (samples * proj_rank * proj_rank) + epsilon
    system = gram_matrix / samples + damping * jnp.eye(samples, dtype=jnp.float32)
    factor = jnp.linalg.cholesky(system)
    solved = jax.scipy.linalg.cho_solve((factor, True), cross_terms)
    return lax.dynamic_slice_in_dim(solved, lax.axis_index("dp") * seq_count, seq_count, 0)


def solution(mesh):
    in_specs = (
        P("dp", "tensor"),
        P("dp", "tensor"),
        P(None, "tensor"),
        P(None, "tensor"),
        P(None, "tensor", None),
    )
    out_specs = P("dp", None)
    return jax.shard_map(shards, mesh=mesh, in_specs=in_specs, out_specs=out_specs, check_vma=False)
```

profile of v0, /device:TPU:0, one launch (start us, length us, event | category | flops | bytes accessed | tf_op | source)
XLA Modules:
  0.0 116.2 jit_solution(16831811706130720864)
XLA Ops:
  6.5 0.0 copy-start
  6.5 0.0 copy-start.1
  6.5 0.0 reduce-scatter.2.cloned.1.call-start
  6.5 0.0 copy-start.2
  6.5 2.3 %fusion.8 = f32[384,64]{0,1:T(8,128)} fusion(bf16[384,1024]{1,0:T(8,128)(2,1)} %param.5, bf16[64,1024]{1,0:T(8,128)(2,1)} %param.7), kind=kOutput, calls=%fused_computation.17 | convolution fusion | flops 50331648 | bytes 1015808 | tf_op jit(solution)/shard_map/td,rd->tr/dot_general | solution.py:27
  8.8 0.0 reduce-scatter.2.cloned.1.call-update
  8.8 0.0 all-reduce.3.cloned.1.call-start
  8.9 0.0 copy-done.1
  8.9 0.0 copy-done.2
  8.9 1.0 fusion.9
  9.9 0.0 all-reduce.3.cloned.1.call-update
  10.0 21.8 %reduce-scatter.2.cloned.1.call-done = f32[384,16]{0,1:T(8,128)} async-done(((f32[384,64]{0,1:T(8,128)}), f32[384,16]{0,1:T(8,128)}) %reduce-scatter.2.cloned.1.call-update) | async-done | bytes 24592 | tf_op jit(solution)/shard_map/reduce_scatter | solution.py:29
  31.7 0.8 reshape.25
  32.6 34.7 %all-reduce.3.cloned.1.call-done = f32[6,64,64]{2,1,0:T(8,128)} async-done(((f32[6,64,64]{2,1,0:T(8,128)}), f32[6,64,64]{2,1,0:T(8,128)}) %all-reduce.3.cloned.1.call-update) | async-done | bytes 98320 | tf_op jit(solution)/shard_map/psum | solution.py:30
  67.2 1.2 %fusion = f32[6,16,64]{2,1,0:T(8,128)S(1)} fusion(f32[6,64,64]{2,1,0:T(8,128)} %all-reduce.3.cloned.1.call-done, f32[6,64,16]{1,0,2:T(8,128)S(1)} %reshape.25), kind=kOutput, calls=%fused_computation | convolution fusion | flops 4718592 | bytes 147456 | tf_op jit(solution)/shard_map/sti,sto->sio/dot_general | solution.py:32
  68.5 0.1 reshape.29
  68.5 9.2 %all-gather = f32[8,6,1024]{2,1,0:T(8,128)S(1)} all-gather(f32[1,6,1024]{2,1,0:T(8,128)S(1)} %reshape.29), channel_id=1, replica_groups=mesh['dp'=8,'tensor'=4] {'dp'}, dimensions={0}, use_global_device_ids=true | all-gather | bytes 221184 | tf_op jit(solution)/shard_map/all_gather | solution.py:39
  77.7 0.3 fusion.10
  78.1 0.0 copy-done
  78.1 0.6 fusion.11
  78.7 18.8 %all-reduce = (f32[48,256]{1,0:T(8,128)S(1)}, f32[48,48]{1,0:T(8,128)S(1)}) all-reduce(f32[48,256]{1,0:T(8,128)S(1)} %fusion.11, f32[48,48]{1,0:T(8,128)S(1)} %fusion.10), channel_id=1, replica_groups=mesh['dp'=8,'tensor'=4] {'tensor'}, use_global_device_ids=true, to_apply=%region_6.7 | all-reduce | flops 14592 | bytes 116736 | tf_op jit(solution)/shard_map/psum | solution.py:42
  97.5 0.6 select_reduce_fusion.1
  98.8 0.1 copy.14
  98.9 4.4 %cholesky.17 = f32[48,48]{1,0:T(8,128)S(1)} custom-call(f32[48,48]{1,0:T(8,128)S(1)} %fusion.7), custom_call_target="Cholesky" | custom-call | tf_op jit(solution)/shard_map/jit(cholesky)/cholesky | solution.py:47
  103.3 0.6 compare_reduce_fusion
  103.9 0.7 fusion.2
  104.6 3.7 %custom-call.10 = f32[1,48,48]{1,2,0:T(8,128)S(1)} custom-call(f32[1,48,48]{2,1,0:T(8,128)S(1)} %fusion.2), custom_call_target="InvertDiagBlocksLowerTriangular" | custom-call | tf_op jit(solution)/shard_map/jit(_cho_solve)/triangular_solve | solution.py:48
  108.3 0.2 fusion.5
  108.5 0.2 fusion.3
  108.7 0.6 constant_dynamic-slice_fusion
  (4 shorter events, 0.1 us)
Async XLA Ops:
  6.5 71.5 %copy-start = (f32[256,16,64]{0,2,1:T(8,128)S(1)}, f32[256,16,64]{0,2,1:T(8,128)}, u32[]{:S(2)}) copy-start(f32[256,16,64]{0,2,1:T(8,128)} %param.9) | copy-start | bytes 3145732
  6.5 2.4 %copy-start.1 = (bf16[384,1024]{1,0:T(8,128)(2,1)S(1)}, bf16[384,1024]{1,0:T(8,128)(2,1)}, u32[]{:S(2)}) copy-start(bf16[384,1024]{1,0:T(8,128)(2,1)} %param.6) | copy-start | bytes 2359300
  6.5 25.2 %reduce-scatter.2.cloned.1.call-start = ((), (), s32[]{:S(2)}) async-start(), calls=%async_computation.1 | async-start | bytes 122880 | tf_op jit(solution)/shard_map/reduce_scatter | solution.py:29
  6.5 2.4 %copy-start.2 = (bf16[64,1024]{1,0:T(8,128)(2,1)S(1)}, bf16[64,1024]{1,0:T(8,128)(2,1)}, u32[]{:S(2)}) copy-start(bf16[64,1024]{1,0:T(8,128)(2,1)} %param.8) | copy-start | bytes 393220
  8.8 58.4 %all-reduce.3.cloned.1.call-start = ((), (), s32[]{:S(2)}) async-start(), calls=%async_computation.2 | async-start | bytes 393216 | tf_op jit(solution)/shard_map/psum | solution.py:30
Sparse Core Ops, SparseCore 0:
  9.6 22.1 reduce-scatter.1
  34.1 33.1 all-reduce.2
where the time goes:
time: 116 us
  waiting for transfers between devices  56.5 us (49%)
  blocking collectives  28 us (24%)
  between operations  14.2 us (12%)
  other arithmetic  10 us (9%)
  matrix products  5.86 us (5%)
  local copies, waits for them, and re-layouts  1.62 us (1%)
    psum x1, waiting for transfers between devices, shards(): grads_low = lax.psum(grads_part, 'tensor')  34.7 us
    reduce_scatter x1, waiting for transfers between devices, shards(): lax.psum_scatter(inputs_part, 'tensor', scatter_dimension=1, tiled=True)  21.8 us
    psum x1, blocking collectives, shards(): gram_matrix, cross_terms = lax.psum((gram_matrix, cross_terms), 'tensor')  18.8 us
    all_gather x1, blocking collectives, shards(): gathered = lax.all_gather(sample_grads, 'dp', axis=0, tiled=True)  9.17 us
    another operation x3, other arithmetic, shards(): factor = jnp.linalg.cholesky(system)  5.05 us
    another operation x2, other arithmetic, shards(): solved = jax.scipy.linalg.cho_solve((factor, True), cross_terms)  4.32 us
  transfers between devices with their start and end apart: 2, of which 2 were waited for; matrix products, arithmetic and copies ran while one was open for 2% of the time, Pallas kernels for 0%

commit v1 on v0

v1 whole, which is shorter than its diff:
```python
import functools

import jax
import jax.numpy as jnp
from jax import lax
from jax.experimental import pallas as pl
from jax.experimental.pallas import tpu as pltpu
from jax.sharding import PartitionSpec as P

LEN = 64
MESH = pl.DeviceIdType.MESH
NT = (((1,), (1,)), ((), ()))
NN = (((1,), (0,)), ((), ()))

damping_ratio = 0.5
epsilon = 1e-06


def dot32(left, right, dims):
    return lax.dot_general(
        left, right, dims, precision=lax.Precision.HIGHEST, preferred_element_type=jnp.float32
    )


def invert(system, n, width, ref):
    rows = lax.broadcasted_iota(jnp.int32, (n, 2 * width), 0)
    lanes = lax.broadcasted_iota(jnp.int32, (n, 2 * width), 1)
    work = jnp.where(lanes == rows + width, 1.0, system)
    if n <= width and n <= 64:
        for k in range(n):
            column = jnp.broadcast_to(work[:, k : k + 1], work.shape)
            row = work[k : k + 1, :] / column[k : k + 1, :]
            work = jnp.where(rows == k, row, work - column * row)
        return pltpu.roll(work, width, 1)[:, :width]
    ref[...] = work

    def step(k, carry):
        column = jnp.sum(jnp.where(lanes == k, ref[...], 0.0), axis=1, keepdims=True)
        pivot = jnp.sum(jnp.where(rows[:, :1] == k, column, 0.0))
        row = ref[pl.ds(k, 1), :] / pivot
        ref[...] = jnp.where(rows == k, row, ref[...] - column * row)
        return carry

    lax.fori_loop(0, n, step, 0)
    return ref[:, width:]


def kernel(
    n_dp, n_tp, pack,
    attn, ograd, proj_in, proj_out, targets, out,
    a_buf, g_buf, wi, wo, t_buf, t_flat, rs_out, rs_in, a2a_out, a2a_in, s_all,
    gram, cz, c_all, c_mat, inv_ref,
    load_sem, rs_s, rs_r, a2a_s, a2a_r, ag_s, ag_r, gr_s, gr_r, cz_s, cz_r, ca_s, ca_r,
):
    d, z = lax.axis_index("dp"), lax.axis_index("tensor")
    share = rs_out.shape[1]
    rank = proj_in.shape[0]
    per = s_all.shape[0] // n_dp
    n = s_all.shape[0]
    half = s_all.shape[1]
    slots = a2a_out.shape[1] // half

    def each(count, body):
        if count <= 16:
            for k in range(1, count):
                body(k)
        else:
            lax.fori_loop(1, count, lambda k, c: (body(k), c)[1], 0)

    def z_peer(k):
        return lax.rem(z + k, n_tp)

    def d_peer(k):
        return lax.rem(d + k, n_dp)

    barrier = pltpu.get_barrier_semaphore()
    each(n_tp, lambda k: pl.semaphore_signal(barrier, inc=1, device_id=(d, z_peer(k)), device_id_type=MESH))
    each(n_dp, lambda k: pl.semaphore_signal(barrier, inc=1, device_id=(d_peer(k), z), device_id_type=MESH))

    load_pi = pltpu.make_async_copy(proj_in, wi.at[pl.ds(0, rank)], load_sem.at[0])
    load_po = pltpu.make_async_copy(proj_out, wo.at[pl.ds(rank, rank)], load_sem.at[1])
    load_pi.start()
    load_po.start()
    order = [k for k in (2, 3, 1) if k < n_tp] + list(range(4, n_tp)) + [0]
    loads = {}
    for k in order:
        rows = pl.ds(pl.multiple_of(z_peer(k) * share, share), share)
        loads[k] = (
            pltpu.make_async_copy(attn.at[rows], a_buf.at[k], load_sem.at[3 + 2 * k]),
            pltpu.make_async_copy(ograd.at[rows], g_buf.at[k], load_sem.at[4 + 2 * k]),
        )
        for copy in loads[k]:
            copy.start()
    load_t = pltpu.make_async_copy(targets, t_buf, load_sem.at[2])
    load_t.start()
    wi[pl.ds(rank, rank), :] = jnp.zeros((rank, wi.shape[1]), wi.dtype)
    wo[pl.ds(0, rank), :] = jnp.zeros((rank, wo.shape[1]), wo.dtype)
    load_pi.wait()
    load_po.wait()

    def z_copy(src, dst, send, recv, k):
        return pltpu.make_async_remote_copy(
            src_ref=src, dst_ref=dst, send_sem=send, recv_sem=recv,
            device_id=(d, z_peer(k)), device_id_type=MESH,
        )

    def d_copy(src, dst, send, recv, k):
        return pltpu.make_async_remote_copy(
            src_ref=src, dst_ref=dst, send_sem=send, recv_sem=recv,
            device_id=(d_peer(k), z), device_id_type=MESH,
        )

    sends = []

    def rs_copy(k):
        return z_copy(rs_out.at[k], rs_in.at[z], rs_s.at[k], rs_r.at[z], k)

    for position, k in enumerate(order):
        for copy in loads[k]:
            copy.wait()
        part = lax.dot_general(a_buf[k], wi[...], NT, preferred_element_type=jnp.float32)
        part = part + lax.dot_general(g_buf[k], wo[...], NT, preferred_element_type=jnp.float32)
        if k:
            rs_out[k] = part
            if position == 0:
                pl.semaphore_wait(barrier, n_tp + n_dp - 2)
            copy = rs_copy(k)
            copy.start()
            sends.append(copy)
        else:
            rs_in[z] = part

    load_t.wait()
    for r in range(half):
        t_flat[:, pl.ds(r * 2 * rank, 2 * rank)] = jnp.concatenate(
            [t_buf[:, r, :], t_buf[:, r + half, :]], axis=1
        )

    def wait_z(buf, recv):
        for k in range(1, n_tp):
            src = lax.rem(z + n_tp - k, n_tp)
            pltpu.make_async_remote_copy(
                src_ref=buf.at[src], dst_ref=buf.at[src], send_sem=recv.at[src], recv_sem=recv.at[src],
                device_id=(d, src), device_id_type=MESH,
            ).wait_recv()

    wait_z(rs_in, rs_r)
    low = rs_in[0]
    for src in range(1, n_tp):
        low = low + rs_in[src]
    lanes = lax.broadcasted_iota(jnp.int32, low.shape, 1)
    grads = jnp.where(lanes < rank, pltpu.roll(low, rank, 1), low)
    inputs_t = low.T[:rank]
    token = lax.broadcasted_iota(jnp.int32, inputs_t.shape, 1) + z * share
    first = (z * share) // LEN
    left = jnp.concatenate(
        [
            jnp.where((token >= (first + s) * LEN) & (token < (first + s + 1) * LEN), inputs_t, 0.0)
            for s in range(slots)
        ],
        axis=0,
    )
    prods = dot32(left, grads, NN)
    low_lanes = lax.broadcasted_iota(jnp.int32, (half, 2 * rank), 1) < rank
    for q in range(n_tp):
        for s in range(slots):
            base = s * rank + q * 2 * half
            a2a_out[q, s * half : (s + 1) * half, :] = jnp.where(
                low_lanes, prods[base : base + half], prods[base + half : base + 2 * half]
            )
    for k in range(1, n_tp):
        copy = z_copy(a2a_out.at[z_peer(k)], a2a_in.at[z], a2a_s.at[k], a2a_r.at[z], k)
        copy.start()
        sends.append(copy)
    a2a_in[z] = a2a_out[z]
    wait_z(a2a_in, a2a_r)
    mine = [None] * per
    for src in range(n_tp):
        for s in range(slots):
            sample = (src * share) // LEN + s
            if sample * LEN >= (src + 1) * share:
                continue
            term = a2a_in[src, s * half : (s + 1) * half, :]
            mine[sample] = term if mine[sample] is None else mine[sample] + term
    for sample in range(per):
        s_all[d * per + sample] = mine[sample]

    own = pl.ds(d * per, per)

    def ag_copy(k):
        return d_copy(s_all.at[own], s_all.at[own], ag_s.at[k], ag_r.at[d], k)

    each(n_dp, lambda k: ag_copy(k).start())

    own_flat = jnp.concatenate([s_all[own, r, :] for r in range(half)], axis=1)
    cz[z, pl.ds(0, per), :] = dot32(own_flat, t_flat[...], NT)
    if cz.shape[1] > per:
        cz[z, pl.ds(per, cz.shape[1] - per), :] = jnp.zeros((cz.shape[1] - per, cz.shape[2]), jnp.float32)
    for k in range(1, n_tp):
        copy = z_copy(cz.at[z], cz.at[z], cz_s.at[k], cz_r.at[z], k)
        copy.start()
        sends.append(copy)

    def wait_ag(k):
        src = lax.rem(d + n_dp - k, n_dp)
        block = s_all.at[pl.ds(src * per, per)]
        pltpu.make_async_remote_copy(
            src_ref=block, dst_ref=block, send_sem=ag_r.at[src], recv_sem=ag_r.at[src],
            device_id=(src, z), device_id_type=MESH,
        ).wait_recv()

    each(n_dp, wait_ag)
    flat = jnp.concatenate([s_all[:, r, :] for r in range(half)], axis=1)
    width = gram.shape[2]
    if pack:
        pad = jnp.zeros((width // 2 - n, flat.shape[1]), jnp.float32)
        full = dot32(flat, jnp.concatenate([flat, pad, flat, pad], axis=0), NT)
        g_lanes = lax.broadcasted_iota(jnp.int32, (n // 2, width), 1)
        gram[z] = jnp.where(g_lanes < width // 2, full[: n // 2], full[n // 2 :])
    else:
        gram[z] = dot32(flat, flat, NT)
    for k in range(1, n_tp):
        copy = z_copy(gram.at[z], gram.at[z], gr_s.at[k], gr_r.at[z], k)
        copy.start()
        sends.append(copy)

    wait_z(cz, cz_r)
    total = cz[0]
    for src in range(1, n_tp):
        total = total + cz[src]
    c_all[d] = total

    def ca_copy(k):
        return d_copy(c_all.at[d], c_all.at[d], ca_s.at[k], ca_r.at[d], k)

    each(n_dp, lambda k: ca_copy(k).start())

    wait_z(gram, gr_r)
    g_sum = gram[0]
    for src in range(1, n_tp):
        g_sum = g_sum + gram[src]
    if pack:
        g_sum = jnp.concatenate([g_sum, pltpu.roll(g_sum, width // 2, 1)], axis=0)
        system_width = width // 2
        wide = g_sum
    else:
        system_width = width
        wide = jnp.concatenate([g_sum, jnp.zeros_like(g_sum)], axis=1)
    g_rows = lax.broadcasted_iota(jnp.int32, wide.shape, 0)
    g_cols = lax.broadcasted_iota(jnp.int32, wide.shape, 1)
    wide = jnp.where(g_cols < n, wide, 0.0)
    diagonal = g_rows == g_cols
    trace = jnp.sum(jnp.where(diagonal, wide, 0.0))
    damping = damping_ratio * trace / (n * rank * rank) + epsilon
    system = wide / n + jnp.where(diagonal, damping, 0.0)
    inverse = invert(system, n, system_width, inv_ref)
    inv_ref[:, pl.ds(0, system_width)] = inverse

    def wait_ca(k):
        src = lax.rem(d + n_dp - k, n_dp)
        block = c_all.at[src]
        pltpu.make_async_remote_copy(
            src_ref=block, dst_ref=block, send_sem=ca_r.at[src], recv_sem=ca_r.at[src],
            device_id=(src, z), device_id_type=MESH,
        ).wait_recv()

    each(n_dp, wait_ca)
    for q in range(n_dp):
        c_mat[q * per : (q + 1) * per, :] = c_all[q, :per, :]
    weights = jnp.concatenate([inv_ref[pl.ds(d * per + i, 1), :] for i in range(per)], axis=0)[:, :n]
    out[...] = dot32(weights, c_mat[...], NN)

    for copy in sends:
        copy.wait_send()
    each(n_dp, lambda k: ag_copy(k).wait_send())
    each(n_dp, lambda k: ca_copy(k).wait_send())


def shards(n_dp, n_tp, attn_out, out_grad, proj_in, proj_out, targets):
    tokens, model = attn_out.shape
    rank = proj_in.shape[0]
    n_targets, part_width, _ = targets.shape
    per = tokens // LEN
    n = per * n_dp
    share = tokens // n_tp
    half = part_width // 2
    slots = max(-(-((q + 1) * share) // LEN) - (q * share) // LEN for q in range(n_tp))
    pack = n <= rank and n % 16 == 0 and rank == 64
    padded = -(-per // 8) * 8
    gram_shape = (n_tp, n // 2, 2 * rank) if pack else (n_tp, n, n)
    inv_width = 2 * rank if pack else 2 * n
    f32, dma = jnp.float32, pltpu.SemaphoreType.DMA
    any_spec = pl.BlockSpec(memory_space=pl.ANY)
    return pl.pallas_call(
        functools.partial(kernel, n_dp, n_tp, pack),
        out_shape=jax.ShapeDtypeStruct((per, n_targets), f32),
        in_specs=[any_spec] * 5,
        out_specs=pl.BlockSpec(memory_space=pltpu.VMEM),
        scratch_shapes=[
            pltpu.VMEM((n_tp, share, model), attn_out.dtype),
            pltpu.VMEM((n_tp, share, model), out_grad.dtype),
            pltpu.VMEM((2 * rank, model), proj_in.dtype),
            pltpu.VMEM((2 * rank, model), proj_out.dtype),
            pltpu.VMEM(targets.shape, f32),
            pltpu.VMEM((n_targets, part_width * rank), f32),
            pltpu.VMEM((n_tp, share, 2 * rank), f32),
            pltpu.VMEM((n_tp, share, 2 * rank), f32),
            pltpu.VMEM((n_tp, slots * half, 2 * rank), f32),
            pltpu.VMEM((n_tp, slots * half, 2 * rank), f32),
            pltpu.VMEM((n, half, 2 * rank), f32),
            pltpu.VMEM(gram_shape, f32),
            pltpu.VMEM((n_tp, padded, n_targets), f32),
            pltpu.VMEM((n_dp, padded, n_targets), f32),
            pltpu.VMEM((n, n_targets), f32),
            pltpu.VMEM((n, inv_width), f32),
            dma((3 + 2 * n_tp,)),
        ]
        + [dma((n_tp,))] * 4
        + [dma((n_dp,))] * 2
        + [dma((n_tp,))] * 4
        + [dma((n_dp,))] * 2,
        compiler_params=pltpu.CompilerParams(
            collective_id=0, has_side_effects=True, vmem_limit_bytes=60 * 1024 * 1024
        ),
    )(attn_out, out_grad, proj_in, proj_out, targets)


def solution(mesh):
    in_specs = (
        P("dp", "tensor"),
        P("dp", "tensor"),
        P(None, "tensor"),
        P(None, "tensor"),
        P(None, "tensor", None),
    )
    return jax.shard_map(
        functools.partial(shards, mesh.shape["dp"], mesh.shape["tensor"]),
        mesh=mesh, in_specs=in_specs, out_specs=P("dp", None), check_vma=False,
    )
```

time: 116 us -> 34.2 us (0.29)
  waiting for transfers between devices: 56.5 us -> 0 us
  Pallas kernels: 0 us -> 29 us
  blocking collectives: 28 us -> 0 us
  between operations: 14.2 us -> 0.01 us
  other arithmetic: 10 us -> 0 us
  matrix products: 5.86 us -> 0 us
  local copies, waits for them, and re-layouts: 1.62 us -> 5.02 us
    psum x1 -> x0, waiting for transfers between devices: 34.7 us -> none  [shards(): grads_low = lax.psum(grads_part, 'tensor')]
    pallas_call x0 -> x1, Pallas kernels: none -> 29 us  [shards(): pl.pallas_call(functools.partial(kernel, n_dp, n_tp, pack), out_shape=jax...]
    reduce_scatter x1 -> x0, waiting for transfers between devices: 21.8 us -> none  [shards(): lax.psum_scatter(inputs_part, 'tensor', scatter_dimension=1, tiled=True)]
    psum x1 -> x0, blocking collectives: 18.8 us -> none  [shards(): gram_matrix, cross_terms = lax.psum((gram_matrix, cross_terms), 'tensor')]
    another operation x5 -> x0, other arithmetic: 9.37 us -> none  [the longest x3 5.05 us: shards(): factor = jnp.linalg.cholesky(system)]
    all_gather x1 -> x0, blocking collectives: 9.17 us -> none  [shards(): gathered = lax.all_gather(sample_grads, 'dp', axis=0, tiled=True)]
    unnamed x8 -> x2, local copies, waits for them, and re-layouts: 0.12 us -> 5.02 us
    dot_general x4 -> x0, matrix products: 4.4 us -> none  [the longest x1 2.28 us: shards(): jnp.einsum('td,rd->tr', attn_out, proj_in, preferred_element_type=jnp.flo...]
  transfers between devices with their start and end apart: 2 -> 0, of which waited for: 2 -> 0; matrix products, arithmetic and copies ran while one was open for 2% -> 0% of each run, Pallas kernels for 0% -> 0%
where the time goes in v1:
time: 34.2 us; the launch traced here: 34 us
  Pallas kernels  29 us (85%)
  local copies, waits for them, and re-layouts  5.02 us (15%)
    pallas_call x1, Pallas kernels, shards(): pl.pallas_call(functools.partial(kernel, n_dp, n_tp, pack), out_shape=jax...  29 us
    unnamed x2, local copies, waits for them, and re-layouts  5.02 us

profile of v1, /device:TPU:0, one launch (start us, length us, event | category | flops | bytes accessed | tf_op | source)
XLA Modules:
  0.0 34.0 jit_solution(2802875881238702257)
XLA Ops:
  0.0 3.7 %copy.6.targets = f32[256,16,64]{2,1,0:T(8,128)} copy(f32[256,16,64]{0,2,1:T(8,128)} %param.9) | data formatting | bytes 2097152 | tf_op args[4]
  3.7 29.0 %shard_map.55 = f32[6,256]{1,0:T(8,128)} custom-call(bf16[384,1024]{1,0:T(8,128)(2,1)} %attn.1, bf16[384,1024]{1,0:T(8,128)(2,1)} %ograd.1, bf16[64,1024]{1,0:T(8,128)(2,1)} %proj_in.1, bf16[64,1024]{1,0:T(8,128)(2,1)} %proj_out.1, f32[256,16,64]{2,1,0:T(8,128)} %copy.6.targets), custom_call_target="tpu_custom_call" | custom-call | tf_op jit(solution)/shard_map/pallas_call | solution.py:294
  32.8 1.3 %copy.8 = f32[6,256]{1,0:T(8,128)} copy(f32[6,256]{1,0:T(8,128)} %shard_map.55) | data formatting | bytes 12288

commit v2 on v1

--- a/solution.py
+++ b/solution.py
@@ -26,11 +26,17 @@
     rows = lax.broadcasted_iota(jnp.int32, (n, 2 * width), 0)
     lanes = lax.broadcasted_iota(jnp.int32, (n, 2 * width), 1)
     work = jnp.where(lanes == rows + width, 1.0, system)
-    if n <= width and n <= 64:
-        for k in range(n):
-            column = jnp.broadcast_to(work[:, k : k + 1], work.shape)
-            row = work[k : k + 1, :] / column[k : k + 1, :]
-            work = jnp.where(rows == k, row, work - column * row)
+    if n <= width and n <= 64 and n % 2 == 0:
+        for k in range(0, n, 2):
+            one = jnp.broadcast_to(work[:, k : k + 1], work.shape)
+            two = jnp.broadcast_to(work[:, k + 1 : k + 2], work.shape)
+            top, low = work[k : k + 1, :], work[k + 1 : k + 2, :]
+            scale = 1.0 / one[k : k + 1, :]
+            cross, ratio = two[k : k + 1, :], one[k + 1 : k + 2, :] * scale
+            second = (low - ratio * top) / (two[k + 1 : k + 2, :] - ratio * cross)
+            first = (top - cross * second) * scale
+            rest = work - one * first - two * second
+            work = jnp.where(rows == k, first, jnp.where(rows == k + 1, second, rest))
         return pltpu.roll(work, width, 1)[:, :width]
     ref[...] = work
 
@@ -48,7 +54,7 @@
 def kernel(
     n_dp, n_tp, pack,
     attn, ograd, proj_in, proj_out, targets, out,
-    a_buf, g_buf, wi, wo, t_buf, t_flat, rs_out, rs_in, a2a_out, a2a_in, s_all,
+    a_buf, g_buf, wi, wo, t_buf, rs_out, rs_in, a2a_out, a2a_in, s_all,
     gram, cz, c_all, c_mat, inv_ref,
     load_sem, rs_s, rs_r, a2a_s, a2a_r, ag_s, ag_r, gr_s, gr_r, cz_s, cz_r, ca_s, ca_r,
 ):
@@ -129,12 +135,6 @@
             sends.append(copy)
         else:
             rs_in[z] = part
-
-    load_t.wait()
-    for r in range(half):
-        t_flat[:, pl.ds(r * 2 * rank, 2 * rank)] = jnp.concatenate(
-            [t_buf[:, r, :], t_buf[:, r + half, :]], axis=1
-        )
 
     def wait_z(buf, recv):
         for k in range(1, n_tp):
@@ -193,7 +193,9 @@
     each(n_dp, lambda k: ag_copy(k).start())
 
     own_flat = jnp.concatenate([s_all[own, r, :] for r in range(half)], axis=1)
-    cz[z, pl.ds(0, per), :] = dot32(own_flat, t_flat[...], NT)
+    load_t.wait()
+    target_cols = jnp.concatenate([t_buf[i] for r in range(half) for i in (r, r + half)], axis=0)
+    cz[z, pl.ds(0, per), :] = dot32(own_flat, target_cols, NN)
     if cz.shape[1] > per:
         cz[z, pl.ds(per, cz.shape[1] - per), :] = jnp.zeros((cz.shape[1] - per, cz.shape[2]), jnp.float32)
     for k in range(1, n_tp):
@@ -301,8 +303,7 @@
             pltpu.VMEM((n_tp, share, model), out_grad.dtype),
             pltpu.VMEM((2 * rank, model), proj_in.dtype),
             pltpu.VMEM((2 * rank, model), proj_out.dtype),
-            pltpu.VMEM(targets.shape, f32),
-            pltpu.VMEM((n_targets, part_width * rank), f32),
+            pltpu.VMEM((part_width, rank, n_targets), f32),
             pltpu.VMEM((n_tp, share, 2 * rank), f32),
             pltpu.VMEM((n_tp, share, 2 * rank), f32),
             pltpu.VMEM((n_tp, slots * half, 2 * rank), f32),
@@ -322,7 +323,7 @@
         compiler_params=pltpu.CompilerParams(
             collective_id=0, has_side_effects=True, vmem_limit_bytes=60 * 1024 * 1024
         ),
-    )(attn_out, out_grad, proj_in, proj_out, targets)
+    )(attn_out, out_grad, proj_in, proj_out, jnp.transpose(targets, (1, 2, 0)))
 
 
 def solution(mesh):

time: 34.2 us -> 29.3 us (0.86)
  local copies, waits for them, and re-layouts: 5.02 us -> 1.3 us
  Pallas kernels: 29 us -> 27.7 us
    unnamed x2 -> x1, local copies, waits for them, and re-layouts: 5.02 us -> 1.3 us
    pallas_call x1, Pallas kernels: 29 us -> 27.7 us  [shards(): pl.pallas_call(functools.partial(kernel, n_dp, n_tp, pack), out_shape=jax...]
where the time goes in v2:
time: 29.3 us; the launch traced here: 29.1 us
  Pallas kernels  27.7 us (95%)
  local copies, waits for them, and re-layouts  1.3 us (4%)
    pallas_call x1, Pallas kernels, shards(): pl.pallas_call(functools.partial(kernel, n_dp, n_tp, pack), out_shape=jax...  27.7 us
    unnamed x1, local copies, waits for them, and re-layouts  1.3 us

profile of v2, /device:TPU:0, one launch (start us, length us, event | category | flops | bytes accessed | tf_op | source)
XLA Modules:
  0.0 29.1 jit_solution(10701634096207669655)
XLA Ops:
  0.0 27.7 %shard_map.55 = f32[6,256]{1,0:T(8,128)} custom-call(bf16[384,1024]{1,0:T(8,128)(2,1)} %attn.1, bf16[384,1024]{1,0:T(8,128)(2,1)} %ograd.1, bf16[64,1024]{1,0:T(8,128)(2,1)} %proj_in.1, bf16[64,1024]{1,0:T(8,128)(2,1)} %proj_out.1, f32[16,64,256]{2,1,0:T(8,128)} %bitcast.1), custom_call_target="tpu_custom_call" | custom-call | tf_op jit(solution)/shard_map/pallas_call | solution.py:296
  27.8 1.3 %copy.7 = f32[6,256]{1,0:T(8,128)} copy(f32[6,256]{1,0:T(8,128)} %shard_map.55) | data formatting | bytes 12288
